TPU v7x, 32 devices: a whole 2x2x4 slice. The times are simulated.
32 devices in a mesh: dp: 8 (over y, x, core), mp: 4 (over z).
Axes of the slice: x: 2, y: 2, z: 4, core: 2. Of those that a mesh axis runs over, the one named last changes fastest.
Arguments:
- hidden_in: bfloat16 [4096, 2048], P('dp'), may hold values from -6 to 6
- cotangent: bfloat16 [4096, 2048], P('dp'), may hold values from -6 to 6
- segments: int32 [8, 512], P('dp'), may hold values from 0 to 5, never falling along the last dimension, each value on 1 to 256 neighbouring positions
- live_counts: int32 [8], P('dp'), may hold values from 128 to 512, as said below
- w_query: bfloat16 [2048, 2048], P('dp', 'mp'), may hold values from -0.125 to 0.125
- w_key: bfloat16 [2048, 2048], P('dp', 'mp'), may hold values from -0.125 to 0.125
- w_value: bfloat16 [2048, 2048], P('dp', 'mp'), may hold values from -0.125 to 0.125
- w_output: bfloat16 [2048, 2048], P('mp', 'dp'), may hold values from -0.125 to 0.125
- w_gate: bfloat16 [2048, 8192], P('dp', 'mp'), may hold values from -0.125 to 0.125
- w_up: bfloat16 [2048, 8192], P('dp', 'mp'), may hold values from -0.125 to 0.125
- w_down: bfloat16 [8192, 2048], P('mp', 'dp'), may hold values from -0.0625 to 0.0625
- query_gain: float32 [2048], P('mp'), may hold values from 0.5 to 1.5
- key_gain: float32 [2048], P('mp'), may hold values from 0.5 to 1.5
- attn_gain: float32 [2048], replicated, may hold values from 0.5 to 1.5
- ffn_gain: float32 [2048], replicated, may hold values from 0.5 to 1.5
Outputs:
- hidden_out: bfloat16 [4096, 2048], P('dp')
- grad_in: float32 [4096, 2048], P('dp')
- grad_query: float32 [2048, 2048], P('dp', 'mp')
- grad_key: float32 [2048, 2048], P('dp', 'mp')
- grad_value: float32 [2048, 2048], P('dp', 'mp')
- grad_output_w: float32 [2048, 2048], P('mp', 'dp')
- grad_gate: float32 [2048, 8192], P('dp', 'mp')
- grad_up: float32 [2048, 8192], P('dp', 'mp')
- grad_down: float32 [8192, 2048], P('mp', 'dp')
- grad_query_gain: float32 [2048], P('mp')
- grad_key_gain: float32 [2048], P('mp')
- grad_attn_gain: float32 [2048], replicated
- grad_ffn_gain: float32 [2048], replicated
Inputs may be any that keep to these rules, and one draw needn't show every extreme that they name: Within the rows of one index of dp, segments never fall; each of the 6 documents has 1 to 256 rows and one has exactly 256. `live_counts`: rows of a block at or after its live count are padding; some index of dp has 512 live rows and some has 128.
All inputs are finite; a program needn't handle non-finite values.
Results may differ from a plain program's by a relative error of at most 0.017.
Values may be sent and summed in bfloat16 or wider, within the bound.
A program may use at most 256 MiB of HBM per device.

v0:
```python
import math
import jax
import jax.numpy as jnp
from jax import lax
from jax.sharding import PartitionSpec as P

HD = 128
EPS = 1e-06
THETA = 500000.0


def doc_positions(seg_row):
    row_count = seg_row.shape[0]
    row_index = jnp.arange(row_count, dtype=jnp.int32)
    change = jnp.concatenate([jnp.ones((1,), dtype=bool), seg_row[1:] != seg_row[:-1]])
    doc_start = lax.cummax(jnp.where(change, row_index, jnp.zeros_like(row_index)), axis=0)
    return (row_index - doc_start).astype(jnp.float32)


def rotary_tables(positions, head_size):
    half_size = head_size // 2
    inv_freq = THETA ** (-(jnp.arange(half_size, dtype=jnp.float32) * (2.0 / head_size)))
    angles = positions[:, None] * inv_freq[None, :]
    return (jnp.cos(angles)[:, None, :], jnp.sin(angles)[:, None, :])


def rotate(values, cos_tab, sin_tab):
    half_size = values.shape[2] // 2
    first_half = values[:, :, :half_size]
    second_half = values[:, :, half_size:]
    return jnp.concatenate(
        [
            first_half * cos_tab - second_half * sin_tab,
            second_half * cos_tab + first_half * sin_tab,
        ],
        axis=2,
    )


def rotate_back(grads, cos_tab, sin_tab):
    half_size = grads.shape[2] // 2
    first_half = grads[:, :, :half_size]
    second_half = grads[:, :, half_size:]
    return jnp.concatenate(
        [
            first_half * cos_tab + second_half * sin_tab,
            second_half * cos_tab - first_half * sin_tab,
        ],
        axis=2,
    )


def block_mask(seg_row, offset, block_rows):
    row_index = jnp.arange(seg_row.shape[0])
    same = seg_row[offset : offset + block_rows, None] == seg_row[None, :]
    return same & (row_index[:, None] >= row_index[None, :])


def block_scores(q_blk, k_bf, allowed, score_scale):
    scores = (
        jnp.einsum("qhe,khe->hqk", q_blk, k_bf, preferred_element_type=jnp.float32) * score_scale
    )
    return jnp.where(allowed[None], scores, jnp.float32(-1e30))


def attend_forward(q_bf, k_bf, v_bf, seg_row, score_scale):
    row_count = q_bf.shape[0]
    block_rows = min(512, row_count)
    allowed = block_mask(seg_row, 0, block_rows)
    scores = block_scores(q_bf, k_bf, allowed, score_scale)
    row_max = jnp.max(scores, axis=2, keepdims=True)
    lse = row_max + jnp.log(jnp.sum(jnp.exp(scores - row_max), axis=2, keepdims=True))
    probs = jnp.exp(scores - lse).astype(jnp.bfloat16)
    outputs = jnp.einsum("hqk,khe->qhe", probs, v_bf, preferred_element_type=jnp.float32)
    lse_parts = [lse]
    return (outputs.astype(jnp.bfloat16), lse_parts)


def attend_backward(q_bf, k_bf, v_bf, o_bf, do_bf, lse_parts, seg_row, score_scale):
    row_count = q_bf.shape[0]
    block_rows = min(512, row_count)
    dq_parts = []
    dk_acc = jnp.zeros(k_bf.shape, jnp.float32)
    dv_acc = jnp.zeros(v_bf.shape, jnp.float32)
    for part_index, offset in enumerate(range(0, row_count, block_rows)):
        allowed = block_mask(seg_row, offset, block_rows)
        scores = block_scores(q_bf, k_bf, allowed, score_scale)
        probs = jnp.exp(scores - lse_parts[part_index])
        probs_bf = probs.astype(jnp.bfloat16)
        dprob = jnp.einsum("qhe,khe->hqk", do_bf, v_bf, preferred_element_type=jnp.float32)
        delta = jnp.transpose(
            jnp.sum(do_bf.astype(jnp.float32) * o_bf.astype(jnp.float32), axis=2)
        )[:, :, None]
        dscore = (probs * (dprob - delta)).astype(jnp.bfloat16)
        dq_parts.append(
            jnp.einsum("hqk,khe->qhe", dscore, k_bf, preferred_element_type=jnp.float32)
            * score_scale
        )
        dk_acc = (
            jnp.einsum("hqk,qhe->khe", dscore, q_bf, preferred_element_type=jnp.float32)
            * score_scale
        )
        dv_acc = jnp.einsum("hqk,qhe->khe", probs_bf, do_bf, preferred_element_type=jnp.float32)
    return (dq_parts[0], dk_acc, dv_acc.astype(jnp.bfloat16))


def scatter_grad(grad, axis_name, scatter_dimension, tiled):
    total = lax.psum_scatter(
        grad.astype(jnp.bfloat16), axis_name, scatter_dimension=scatter_dimension, tiled=tiled
    )
    return total.astype(jnp.float32)


def sum_parts(part, axis_name):
    own = lax.psum_scatter(part.astype(jnp.bfloat16), axis_name, scatter_dimension=0, tiled=True)
    return lax.all_gather(own, axis_name, axis=0, tiled=True).astype(jnp.float32)


def norm_back(raw, inv_scale, gained, row_sums, width):
    return inv_scale * gained - raw * inv_scale**3 * (row_sums[:, None] / width)


def on_device(
    hidden_in,
    cotangent,
    segments,
    live_counts,
    w_query,
    w_key,
    w_value,
    w_output,
    w_gate,
    w_up,
    w_down,
    query_gain,
    key_gain,
    attn_gain,
    ffn_gain,
):
    gathered = (
        lax.all_gather(w_query, "dp", axis=0, tiled=True),
        lax.all_gather(w_key, "dp", axis=0, tiled=True),
        lax.all_gather(w_value, "dp", axis=0, tiled=True),
        lax.all_gather(w_output, "dp", axis=1, tiled=True),
        lax.all_gather(w_gate, "dp", axis=0, tiled=True),
        lax.all_gather(w_up, "dp", axis=0, tiled=True),
        lax.all_gather(w_down, "dp", axis=1, tiled=True),
    )
    wq_full, wk_full, wv_full, wo_full, wg_full, wu_full, wd_full = gathered
    seg_row = segments[0]
    live_n = live_counts[0]
    row_count, width = hidden_in.shape
    local_width = wq_full.shape[1]
    heads_here = local_width // HD
    score_scale = 1.0 / math.sqrt(HD)
    live_mask = (jnp.arange(row_count, dtype=jnp.int32) < live_n).astype(jnp.float32)[:, None]
    cos_tab, sin_tab = rotary_tables(doc_positions(seg_row), HD)
    q_proj = jnp.dot(hidden_in, wq_full, preferred_element_type=jnp.float32)
    k_proj = jnp.dot(hidden_in, wk_full, preferred_element_type=jnp.float32)
    v_bf = jnp.dot(hidden_in, wv_full, preferred_element_type=jnp.float32).astype(jnp.bfloat16)
    sq_query, sq_key = lax.psum(
        (jnp.sum(q_proj * q_proj, axis=1), jnp.sum(k_proj * k_proj, axis=1)), "mp"
    )
    inv_q = lax.rsqrt(sq_query[:, None] / width + EPS)
    inv_k = lax.rsqrt(sq_key[:, None] / width + EPS)
    q_rot = rotate(
        (q_proj * inv_q * query_gain).reshape(row_count, heads_here, HD), cos_tab, sin_tab
    ).astype(jnp.bfloat16)
    k_rot = rotate(
        (k_proj * inv_k * key_gain).reshape(row_count, heads_here, HD), cos_tab, sin_tab
    ).astype(jnp.bfloat16)
    v_heads = v_bf.reshape(row_count, heads_here, HD)
    o_bf, lse_parts = attend_forward(q_rot, k_rot, v_heads, seg_row, score_scale)
    o_flat = o_bf.reshape(row_count, local_width)
    attn_raw = sum_parts(jnp.dot(o_flat, wo_full, preferred_element_type=jnp.float32), "mp")
    inv_a = lax.rsqrt(jnp.mean(attn_raw * attn_raw, axis=1, keepdims=True) + EPS)
    h_mid = hidden_in.astype(jnp.float32) + attn_raw * inv_a * attn_gain
    h_bf = h_mid.astype(jnp.bfloat16)
    gate_pre = jnp.dot(h_bf, wg_full, preferred_element_type=jnp.float32)
    up_pre = jnp.dot(h_bf, wu_full, preferred_element_type=jnp.float32)
    act_bf = (jax.nn.silu(gate_pre) * up_pre).astype(jnp.bfloat16)
    ffn_raw = sum_parts(jnp.dot(act_bf, wd_full, preferred_element_type=jnp.float32), "mp")
    inv_f = lax.rsqrt(jnp.mean(ffn_raw * ffn_raw, axis=1, keepdims=True) + EPS)
    hidden_out = (live_mask * (h_mid + ffn_raw * inv_f * ffn_gain)).astype(jnp.bfloat16)
    wq_back, wk_back, wv_back, wo_back, wg_back, wu_back, wd_back = gathered
    dy = live_mask * cotangent.astype(jnp.float32)
    g_ffn_gain = jnp.sum(dy * ffn_raw * inv_f, axis=0)
    gained_f = ffn_gain * dy
    d_ffn = norm_back(ffn_raw, inv_f, gained_f, jnp.sum(gained_f * ffn_raw, axis=1), width).astype(
        jnp.bfloat16
    )
    d_act = jnp.dot(d_ffn, wd_back.T, preferred_element_type=jnp.float32)
    sig = jax.nn.sigmoid(gate_pre)
    d_up = (d_act * gate_pre * sig).astype(jnp.bfloat16)
    d_gate = (d_act * up_pre * sig * (1.0 + gate_pre * (1.0 - sig))).astype(jnp.bfloat16)
    ffn_part = jnp.dot(d_gate, wg_back.T, preferred_element_type=jnp.float32) + jnp.dot(
        d_up, wu_back.T, preferred_element_type=jnp.float32
    )
    dh = dy + sum_parts(ffn_part, "mp")
    g_down = jnp.dot(act_bf.T, d_ffn, preferred_element_type=jnp.float32)
    g_gate = jnp.dot(h_bf.T, d_gate, preferred_element_type=jnp.float32)
    g_up = jnp.dot(h_bf.T, d_up, preferred_element_type=jnp.float32)
    g_attn_gain = jnp.sum(dh * attn_raw * inv_a, axis=0)
    gained_a = attn_gain * dh
    d_attn = norm_back(
        attn_raw, inv_a, gained_a, jnp.sum(gained_a * attn_raw, axis=1), width
    ).astype(jnp.bfloat16)
    d_heads = jnp.dot(d_attn, wo_back.T, preferred_element_type=jnp.float32).astype(jnp.bfloat16)
    g_output = jnp.dot(o_flat.T, d_attn, preferred_element_type=jnp.float32)
    dq_rot, dk_rot, d_val = attend_backward(
        q_rot,
        k_rot,
        v_heads,
        o_bf,
        d_heads.reshape(row_count, heads_here, HD),
        lse_parts,
        seg_row,
        score_scale,
    )
    dq_norm = rotate_back(dq_rot, cos_tab, sin_tab).reshape(row_count, local_width)
    dk_norm = rotate_back(dk_rot, cos_tab, sin_tab).reshape(row_count, local_width)
    g_query_gain = jnp.sum(dq_norm * q_proj * inv_q, axis=0)
    g_key_gain = jnp.sum(dk_norm * k_proj * inv_k, axis=0)
    gained_q = query_gain * dq_norm
    gained_k = key_gain * dk_norm
    sums_query, sums_key = lax.psum(
        (jnp.sum(gained_q * q_proj, axis=1), jnp.sum(gained_k * k_proj, axis=1)), "mp"
    )
    dq_bf = norm_back(q_proj, inv_q, gained_q, sums_query, width).astype(jnp.bfloat16)
    dk_bf = norm_back(k_proj, inv_k, gained_k, sums_key, width).astype(jnp.bfloat16)
    dv_bf = d_val.reshape(row_count, local_width)
    input_part = (
        jnp.dot(dq_bf, wq_back.T, preferred_element_type=jnp.float32)
        + jnp.dot(dk_bf, wk_back.T, preferred_element_type=jnp.float32)
        + jnp.dot(dv_bf, wv_back.T, preferred_element_type=jnp.float32)
    )
    grad_in = dh + sum_parts(input_part, "mp")
    g_query = jnp.dot(hidden_in.T, dq_bf, preferred_element_type=jnp.float32)
    g_key = jnp.dot(hidden_in.T, dk_bf, preferred_element_type=jnp.float32)
    g_value = jnp.dot(hidden_in.T, dv_bf, preferred_element_type=jnp.float32)
    owned = (
        scatter_grad(g_query, "dp", scatter_dimension=0, tiled=True),
        scatter_grad(g_key, "dp", scatter_dimension=0, tiled=True),
        scatter_grad(g_value, "dp", scatter_dimension=0, tiled=True),
        scatter_grad(g_output, "dp", scatter_dimension=1, tiled=True),
        scatter_grad(g_gate, "dp", scatter_dimension=0, tiled=True),
        scatter_grad(g_up, "dp", scatter_dimension=0, tiled=True),
        scatter_grad(g_down, "dp", scatter_dimension=1, tiled=True),
    )
    gain_totals = lax.psum((g_query_gain, g_key_gain, g_attn_gain, g_ffn_gain), "dp")
    return (
        hidden_out,
        grad_in,
        owned[0],
        owned[1],
        owned[2],
        owned[3],
        owned[4],
        owned[5],
        owned[6],
        gain_totals[0],
        gain_totals[1],
        gain_totals[2],
        gain_totals[3],
    )


def solution(mesh):
    return jax.shard_map(
        on_device,
        mesh=mesh,
        in_specs=(
            P("dp", None),
            P("dp", None),
            P("dp", None),
            P("dp"),
            P("dp", "mp"),
            P("dp", "mp"),
            P("dp", "mp"),
            P("mp", "dp"),
            P("dp", "mp"),
            P("dp", "mp"),
            P("mp", "dp"),
            P("mp"),
            P("mp"),
            P(),
            P(),
        ),
        out_specs=(
            P("dp", None),
            P("dp", None),
            P("dp", "mp"),
            P("dp", "mp"),
            P("dp", "mp"),
            P("mp", "dp"),
            P("dp", "mp"),
            P("dp", "mp"),
            P("mp", "dp"),
            P("mp"),
            P("mp"),
            P(),
            P(),
        ),
        check_vma=False,
    )
```

profile of v0, /device:TPU:0, one launch (start us, length us, event | category | flops | bytes accessed | tf_op | source)
XLA Modules:
  0.0 1167.2 jit_solution(17144449254800355425)
XLA Ops:
  14.4 26.0 %all-gather.16.cloned.1.call-done = bf16[2048,512]{1,0:T(8,128)(2,1)} async-done(((bf16[256,512]{1,0:T(8,128)(2,1)}), bf16[2048,512]{1,0:T(8,128)(2,1)}) %all-gather.16.cloned.1.call-update) | async-done | bytes 2097168 | tf_op jit(solution)/shard_map/all_gather | solution.py:142
  40.4 3.5 multiply_reduce_fusion.3
  44.0 26.1 %all-gather.14.cloned.1.call-done = bf16[2048,512]{1,0:T(8,128)(2,1)} async-done(((bf16[256,512]{1,0:T(8,128)(2,1)}), bf16[2048,512]{1,0:T(8,128)(2,1)}) %all-gather.14.cloned.1.call-update) | async-done | bytes 2097168 | tf_op jit(solution)/shard_map/all_gather | solution.py:141
  70.1 3.5 multiply_reduce_fusion.4
  73.7 11.7 %all-reduce.2 = (f32[512]{0:T(512)S(1)}, f32[512]{0:T(512)S(1)}) all-reduce(f32[512]{0:T(512)S(1)} %get-tuple-element.85, f32[512]{0:T(512)S(1)} %get-tuple-element.87), channel_id=1, replica_groups=mesh['dp'=8,'mp'=4] {'mp'}, use_global_device_ids=true, to_apply=%region_5.6 | all-reduce | flops 1024 | bytes 8192 | tf_op jit(solution)/shard_map/psum | solution.py:161
  86.6 2.4 copy.82
  89.0 2.4 copy.81
  93.9 2.4 copy.79
  96.3 2.3 subtract_convert_fusion.3
  100.0 2.0 copy-done.7
  103.1 3.0 convolution_convert_fusion.10
  106.9 2.2 convolution_convert_fusion.12
  109.1 20.6 %all-gather.18.cloned.1.call-done = bf16[512,2048]{1,0:T(8,128)(2,1)} async-done(((bf16[512,256]{1,0:T(8,128)(2,1)}), bf16[512,2048]{1,0:T(8,128)(2,1)}) %all-gather.18.cloned.1.call-update) | async-done | bytes 2097168 | tf_op jit(solution)/shard_map/all_gather | solution.py:144
  129.7 4.4 convolution_convert_fusion.8
  134.1 43.7 %reduce-scatter.12.cloned.1.call-done = bf16[128,2048]{1,0:T(8,128)(2,1)} async-done(((bf16[512,2048]{1,0:T(8,128)(2,1)}), bf16[128,2048]{1,0:T(8,128)(2,1)}) %reduce-scatter.12.cloned.1.call-update) | async-done | bytes 524304 | tf_op jit(solution)/shard_map/reduce_scatter | solution.py:115
  180.2 44.0 %all-gather.20.cloned.1.call-done = bf16[512,2048]{1,0:T(8,128)(2,1)} async-done(((bf16[128,2048]{1,0:T(8,128)(2,1)}), bf16[512,2048]{1,0:T(8,128)(2,1)}) %all-gather.20.cloned.1.call-update) | async-done | bytes 2097168 | tf_op jit(solution)/shard_map/all_gather | solution.py:116
  224.2 2.1 fusion
  226.3 4.0 fusion.22
  230.3 48.9 %all-gather.22.cloned.1.call-done = bf16[2048,2048]{1,0:T(8,128)(2,1)} async-done(((bf16[256,2048]{1,0:T(8,128)(2,1)}), bf16[2048,2048]{1,0:T(8,128)(2,1)}) %all-gather.22.cloned.1.call-update) | async-done | bytes 8388624 | tf_op jit(solution)/shard_map/all_gather | solution.py:145
  279.2 10.5 fusion.47
  289.6 45.7 %all-gather.24.cloned.1.call-done = bf16[2048,2048]{1,0:T(8,128)(2,1)} async-done(((bf16[256,2048]{1,0:T(8,128)(2,1)}), bf16[2048,2048]{1,0:T(8,128)(2,1)}) %all-gather.24.cloned.1.call-update) | async-done | bytes 8388624 | tf_op jit(solution)/shard_map/all_gather | solution.py:146
  335.3 10.8 multiply_convert_fusion.3
  346.1 47.0 %all-gather.26.cloned.1.call-done = bf16[2048,2048]{1,0:T(8,128)(2,1)} async-done(((bf16[2048,256]{1,0:T(8,128)(2,1)}), bf16[2048,2048]{1,0:T(8,128)(2,1)}) %all-gather.26.cloned.1.call-update) | async-done | bytes 8388624 | tf_op jit(solution)/shard_map/all_gather | solution.py:147
  393.1 9.8 convolution_convert_fusion.7
  403.0 43.7 %reduce-scatter.14.cloned.1.call-done = bf16[128,2048]{1,0:T(8,128)(2,1)} async-done(((bf16[512,2048]{1,0:T(8,128)(2,1)}), bf16[128,2048]{1,0:T(8,128)(2,1)}) %reduce-scatter.14.cloned.1.call-update) | async-done | bytes 524304 | tf_op jit(solution)/shard_map/reduce_scatter | solution.py:115
  447.7 45.6 %all-gather.28.cloned.1.call-done = bf16[512,2048]{1,0:T(8,128)(2,1)} async-done(((bf16[128,2048]{1,0:T(8,128)(2,1)}), bf16[512,2048]{1,0:T(8,128)(2,1)}) %all-gather.28.cloned.1.call-update) | async-done | bytes 2097168 | tf_op jit(solution)/shard_map/all_gather | solution.py:116
  493.2 2.2 fusion.9
  495.5 3.4 fusion.19
  498.9 11.9 %multiply_convert_fusion.1 = (bf16[512,2048]{1,0:T(8,128)(2,1)}, bf16[512,2048]{1,0:T(8,128)(2,1)}) fusion(f32[512,2048]{1,0:T(8,128)S(1)} %copy-done.45, f32[512,2048]{1,0:T(8,128)} %get-tuple-element.92, bf16[2048,2048]{1,0:T(8,128)(2,1)} %all-gather.26.cloned.1.call-done, bf16[512,2048]{1,0:T(8,128)(2,1)S(1)} %copy-done.5, ...), kind=kOutput, calls=%fused_computation.38 | convolution fusion | flops 4318035968 | bytes 25182208 | tf_op jit(solution)/shard_map/dot_general | solution.py:192
  510.8 7.8 fusion.48
  518.6 9.6 add_convert_fusion.1
  528.2 42.5 %reduce-scatter.16.cloned.1.call-done = bf16[128,2048]{1,0:T(8,128)(2,1)} async-done(((bf16[512,2048]{1,0:T(8,128)(2,1)}), bf16[128,2048]{1,0:T(8,128)(2,1)}) %reduce-scatter.16.cloned.1.call-update) | async-done | bytes 524304 | tf_op jit(solution)/shard_map/reduce_scatter | solution.py:115
  571.0 46.2 %all-gather.30.cloned.1.call-done = bf16[512,2048]{1,0:T(8,128)(2,1)} async-done(((bf16[128,2048]{1,0:T(8,128)(2,1)}), bf16[512,2048]{1,0:T(8,128)(2,1)}) %all-gather.30.cloned.1.call-update) | async-done | bytes 2097168 | tf_op jit(solution)/shard_map/all_gather | solution.py:116
  617.2 4.4 fusion.8
  621.7 5.2 fusion.5
  629.9 2.2 convolution_convert_fusion.11
  636.0 2.0 multiply_add_fusion
  639.0 2.9 pad_maximum_fusion
  641.9 2.5 copy.59
  646.0 10.1 all-reduce.1
  661.5 2.6 add_convert_fusion
  664.2 4.4 convolution_convert_fusion.3
  668.7 2.6 fusion.24
  671.4 2.6 fusion.23
  674.1 4.3 fusion.25
  678.7 10.5 convolution_convert_fusion
  689.2 10.1 convolution_convert_fusion.1
  699.6 10.1 convolution_convert_fusion.2
  710.4 23.1 %all-reduce = (f32[512]{0:T(512)}, f32[512]{0:T(512)}, f32[2048]{0:T(1024)}, f32[2048]{0:T(1024)}) all-reduce(f32[512]{0:T(512)S(1)} %get-tuple-element.45, f32[512]{0:T(512)S(1)} %get-tuple-element.43, f32[2048]{0:T(1024)S(1)} %get-tuple-element.39, f32[2048]{0:T(1024)S(1)} %get-tuple-element.41), channel_id=1, replica_groups=mesh['dp'=8,'mp'=4] {'dp'}, use_global_device_ids=true, to_apply=%region_29.30 | all-reduce | flops 5120 | bytes 40960 | tf_op jit(solution)/shard_map/psum | solution.py:250
  733.5 16.2 %reduce-scatter.26.cloned.1.call-done = bf16[512,256]{1,0:T(8,128)(2,1)} async-done(((bf16[512,2048]{1,0:T(8,128)(2,1)}), bf16[512,256]{1,0:T(8,128)(2,1)}) %reduce-scatter.26.cloned.1.call-update) | async-done | bytes 262160 | tf_op jit(solution)/shard_map/reduce_scatter | solution.py:108
  751.4 42.5 %reduce-scatter.22.cloned.1.call-done = bf16[256,512]{0,1:T(8,128)(2,1)} async-done(((bf16[2048,512]{0,1:T(8,128)(2,1)}), bf16[256,512]{0,1:T(8,128)(2,1)}) %reduce-scatter.22.cloned.1.call-update) | async-done | bytes 262160 | tf_op jit(solution)/shard_map/reduce_scatter | solution.py:108
  794.0 1.9 copy.66
  795.9 42.4 %reduce-scatter.20.cloned.1.call-done = bf16[256,512]{0,1:T(8,128)(2,1)} async-done(((bf16[2048,512]{0,1:T(8,128)(2,1)}), bf16[256,512]{0,1:T(8,128)(2,1)}) %reduce-scatter.20.cloned.1.call-update) | async-done | bytes 262160 | tf_op jit(solution)/shard_map/reduce_scatter | solution.py:108
  838.3 1.9 copy.65
  840.1 42.4 %reduce-scatter.24.cloned.1.call-done = bf16[256,512]{0,1:T(8,128)(2,1)} async-done(((bf16[2048,512]{0,1:T(8,128)(2,1)}), bf16[256,512]{0,1:T(8,128)(2,1)}) %reduce-scatter.24.cloned.1.call-update) | async-done | bytes 262160 | tf_op jit(solution)/shard_map/reduce_scatter | solution.py:108
  882.6 1.9 copy.67
  884.4 72.9 %reduce-scatter.32.cloned.1.call-done = bf16[2048,256]{1,0:T(8,128)(2,1)} async-done(((bf16[2048,2048]{1,0:T(8,128)(2,1)}), bf16[2048,256]{1,0:T(8,128)(2,1)}) %reduce-scatter.32.cloned.1.call-update) | async-done | bytes 1048592 | tf_op jit(solution)/shard_map/reduce_scatter | solution.py:108
  957.3 2.7 convert_element_type.202
  960.1 72.2 %reduce-scatter.30.cloned.1.call-done = bf16[256,2048]{1,0:T(8,128)(2,1)} async-done(((bf16[2048,2048]{1,0:T(8,128)(2,1)}), bf16[256,2048]{1,0:T(8,128)(2,1)}) %reduce-scatter.30.cloned.1.call-update) | async-done | bytes 1048592 | tf_op jit(solution)/shard_map/reduce_scatter | solution.py:108
  1032.2 2.8 convert_element_type.200
  1035.0 72.2 %reduce-scatter.28.cloned.1.call-done = bf16[256,2048]{1,0:T(8,128)(2,1)} async-done(((bf16[2048,2048]{1,0:T(8,128)(2,1)}), bf16[256,2048]{1,0:T(8,128)(2,1)}) %reduce-scatter.28.cloned.1.call-update) | async-done | bytes 1048592 | tf_op jit(solution)/shard_map/reduce_scatter | solution.py:108
  1107.2 2.8 convert_element_type.198
  1110.0 44.5 %all-gather.32.cloned.1.call-done = bf16[512,2048]{1,0:T(8,128)(2,1)} async-done(((bf16[128,2048]{1,0:T(8,128)(2,1)}), bf16[512,2048]{1,0:T(8,128)(2,1)}) %all-gather.32.cloned.1.call-update) | async-done | bytes 2097168 | tf_op jit(solution)/shard_map/all_gather | solution.py:116
  1154.5 5.7 convert_add_fusion
  (178 shorter events, 35.1 us)
Async XLA Ops:
  7.2 33.2 %all-gather.16.cloned.1.call-start = ((), (), s32[]{:S(2)}) async-start(), calls=%async_computation.13 | async-start | bytes 2359296 | tf_op jit(solution)/shard_map/all_gather | solution.py:142
  7.9 62.2 %all-gather.14.cloned.1.call-start = ((), (), s32[]{:S(2)}) async-start(), calls=%async_computation.12 | async-start | bytes 2359296 | tf_op jit(solution)/shard_map/all_gather | solution.py:141
  8.7 94.4 %all-gather.12.cloned.1.call-start = ((), (), s32[]{:S(2)}) async-start(), calls=%async_computation.11 | async-start | bytes 2359296 | tf_op jit(solution)/shard_map/all_gather | solution.py:143
  9.4 120.3 %all-gather.18.cloned.1.call-start = ((), (), s32[]{:S(2)}) async-start(), calls=%async_computation.14 | async-start | bytes 2359296 | tf_op jit(solution)/shard_map/all_gather | solution.py:144
  10.0 167.9 %reduce-scatter.12.cloned.1.call-start = ((), (), s32[]{:S(2)}) async-start(), calls=%async_computation.15 | async-start | bytes 2621440 | tf_op jit(solution)/shard_map/reduce_scatter | solution.py:115
  43.9 41.4 %copy-start.39 = (f32[512]{0:T(512)S(1)}, f32[512]{0:T(512)}, u32[]{:S(2)}) copy-start(f32[512]{0:T(512)} %param.27) | copy-start | bytes 6148
  73.6 17.8 %copy-start.10 = (f32[512,512]{0,1:T(8,128)}, f32[512,512]{0,1:T(8,128)S(1)}, u32[]{:S(2)}) copy-start(f32[512,512]{0,1:T(8,128)S(1)} %get-tuple-element.88) | copy-start | bytes 3145732
  73.7 17.7 %copy-start.38 = (f32[512]{0:T(512)S(1)}, f32[512]{0:T(512)}, u32[]{:S(2)}) copy-start(f32[512]{0:T(512)} %param.26) | copy-start | bytes 6148
  91.5 4.8 copy-start.22
  98.6 4.4 copy-start.14
  98.6 4.4 copy-start.16
  98.6 4.4 copy-start.18
  98.6 4.4 copy-start.20
  98.6 4.4 copy-start.12
  100.0 2.0 copy-start.7
  103.1 3.9 copy-start.8
  134.0 92.2 %copy-start.36 = (f32[2048]{0:T(1024)S(1)}, f32[2048]{0:T(1024)}, u32[]{:S(2)}) copy-start(f32[2048]{0:T(1024)} %param.28) | copy-start | bytes 24580
  134.1 90.1 %all-gather.20.cloned.1.call-start = ((), (), s32[]{:S(2)}) async-start(), calls=%async_computation.16 | async-start | bytes 2621440 | tf_op jit(solution)/shard_map/all_gather | solution.py:116
  177.9 101.3 %all-gather.22.cloned.1.call-start = ((), (), s32[]{:S(2)}) async-start(), calls=%async_computation.17 | async-start | bytes 9437184 | tf_op jit(solution)/shard_map/all_gather | solution.py:145
  178.6 156.7 %all-gather.24.cloned.1.call-start = ((), (), s32[]{:S(2)}) async-start(), calls=%async_computation.18 | async-start | bytes 9437184 | tf_op jit(solution)/shard_map/all_gather | solution.py:146
  179.4 213.7 %all-gather.26.cloned.1.call-start = ((), (), s32[]{:S(2)}) async-start(), calls=%async_computation.19 | async-start | bytes 9437184 | tf_op jit(solution)/shard_map/all_gather | solution.py:147
  180.1 266.6 %reduce-scatter.14.cloned.1.call-start = ((), (), s32[]{:S(2)}) async-start(), calls=%async_computation.20 | async-start | bytes 2621440 | tf_op jit(solution)/shard_map/reduce_scatter | solution.py:115
  230.3 105.1 %copy-start.30 = (bf16[512,2048]{1,0:T(8,128)(2,1)S(1)}, bf16[512,2048]{1,0:T(8,128)(2,1)}, u32[]{:S(2)}) copy-start(bf16[512,2048]{1,0:T(8,128)(2,1)} %fusion.22) | copy-start | bytes 6291460
  402.9 92.5 %copy-start.1 = (bf16[512,2048]{1,0:T(8,128)(2,1)S(1)}, bf16[512,2048]{1,0:T(8,128)(2,1)}, u32[]{:S(2)}) copy-start(bf16[512,2048]{1,0:T(8,128)(2,1)} %param.16) | copy-start | bytes 6291460
  402.9 92.5 %copy-start.37 = (f32[2048]{0:T(1024)S(1)}, f32[2048]{0:T(1024)}, u32[]{:S(2)}) copy-start(f32[2048]{0:T(1024)} %param.29) | copy-start | bytes 24580
  403.0 90.3 %all-gather.28.cloned.1.call-start = ((), (), s32[]{:S(2)}) async-start(), calls=%async_computation.21 | async-start | bytes 2621440 | tf_op jit(solution)/shard_map/all_gather | solution.py:116
  446.8 124.0 %reduce-scatter.16.cloned.1.call-start = ((), (), s32[]{:S(2)}) async-start(), calls=%async_computation.22 | async-start | bytes 2621440 | tf_op jit(solution)/shard_map/reduce_scatter | solution.py:115
  493.2 5.6 copy-start.5
  493.2 5.6 copy-start.45
  510.8 7.8 copy-start.46
  518.6 98.6 %copy-start = (bf16[512,2048]{1,0:T(8,128)(2,1)S(1)}, bf16[512,2048]{1,0:T(8,128)(2,1)}, u32[]{:S(2)}) copy-start(bf16[512,2048]{1,0:T(8,128)(2,1)} %all-gather.20.cloned.1.call-done) | copy-start | bytes 6291460
  528.2 89.0 %all-gather.30.cloned.1.call-start = ((), (), s32[]{:S(2)}) async-start(), calls=%async_computation.23 | async-start | bytes 2621440 | tf_op jit(solution)/shard_map/all_gather | solution.py:116
  570.8 139.0 %reduce-scatter.18.cloned.1.call-start = ((), (), s32[]{:S(2)}) async-start(), calls=%async_computation.24 | async-start | bytes 2621440 | tf_op jit(solution)/shard_map/reduce_scatter | solution.py:115
  617.2 4.4 copy-start.2
  617.2 4.5 copy-start.4
  617.2 4.5 copy-start.6
  621.7 5.3 copy-start.40
  621.7 5.3 copy-start.41
  627.0 5.1 copy-start.33
  627.0 2.9 copy-start.9
  628.4 3.7 copy-start.44
  632.1 1.7 copy-start.19
  632.1 1.7 copy-start.21
  633.8 2.2 copy-start.27
  633.8 2.2 copy-start.28
  638.7 5.7 copy-start.11
  656.1 1.9 copy-start.31
  657.8 1.6 copy-start.23
  658.1 1.8 copy-start.32
  659.8 1.7 copy-start.34
  661.5 2.7 copy-start.42
  664.2 4.5 copy-start.13
  664.2 4.5 copy-start.26
  664.2 85.5 %reduce-scatter.26.cloned.1.call-start = ((), (), s32[]{:S(2)}) async-start(), calls=%async_computation.29 | async-start | bytes 2359296 | tf_op jit(solution)/shard_map/reduce_scatter | solution.py:108
  668.6 2.7 copy-start.24
  668.7 125.3 %reduce-scatter.22.cloned.1.call-start = ((), (), s32[]{:S(2)}) async-start(), calls=%async_computation.27 | async-start | bytes 2359296 | tf_op jit(solution)/shard_map/reduce_scatter | solution.py:108
  671.3 2.7 copy-start.35
  671.3 166.9 %reduce-scatter.20.cloned.1.call-start = ((), (), s32[]{:S(2)}) async-start(), calls=%async_computation.26 | async-start | bytes 2359296 | tf_op jit(solution)/shard_map/reduce_scatter | solution.py:108
  674.0 4.7 copy-start.3
  674.0 208.6 %reduce-scatter.24.cloned.1.call-start = ((), (), s32[]{:S(2)}) async-start(), calls=%async_computation.28 | async-start | bytes 2359296 | tf_op jit(solution)/shard_map/reduce_scatter | solution.py:108
  678.4 278.9 %reduce-scatter.32.cloned.1.call-start = ((), (), s32[]{:S(2)}) async-start(), calls=%async_computation.32 | async-start | bytes 9437184 | tf_op jit(solution)/shard_map/reduce_scatter | solution.py:108
  689.2 343.1 %reduce-scatter.30.cloned.1.call-start = ((), (), s32[]{:S(2)}) async-start(), calls=%async_computation.31 | async-start | bytes 9437184 | tf_op jit(solution)/shard_map/reduce_scatter | solution.py:108
  699.3 407.9 %reduce-scatter.28.cloned.1.call-start = ((), (), s32[]{:S(2)}) async-start(), calls=%async_computation.30 | async-start | bytes 9437184 | tf_op jit(solution)/shard_map/reduce_scatter | solution.py:108
  709.7 444.8 %all-gather.32.cloned.1.call-start = ((), (), s32[]{:S(2)}) async-start(), calls=%async_computation.25 | async-start | bytes 2621440 | tf_op jit(solution)/shard_map/all_gather | solution.py:116
  (5 other events, 5.9 us)
Sparse Core Ops, SparseCore 0:
  9.9 30.4 all-gather.15
  42.3 27.7 all-gather.13
  72.0 27.7 all-gather.11
  101.5 28.0 all-gather.17
  134.2 43.6 reduce-scatter.11
  179.3 44.8 all-gather.19
  226.1 53.0 all-gather.21
  281.0 54.2 all-gather.23
  337.2 55.8 all-gather.25
  403.1 43.6 reduce-scatter.13
  448.3 44.8 all-gather.27
  528.3 42.4 reduce-scatter.15
  572.3 44.8 all-gather.29
  664.3 41.8 reduce-scatter.17
  709.3 40.3 reduce-scatter.25
  752.8 41.1 reduce-scatter.21
  797.1 41.1 reduce-scatter.19
  841.4 41.1 reduce-scatter.23
  886.0 71.2 reduce-scatter.31
  960.7 71.5 reduce-scatter.29
  1035.7 71.4 reduce-scatter.27
  1108.8 45.6 all-gather.31
where the time goes:
time: 1180 us; the launch traced here: 1170 us
  waiting for transfers between devices  891 us (76%)
  matrix products  135 us (11%)
  other arithmetic  53.6 us (5%)
  blocking collectives  44.9 us (4%)
  local copies, waits for them, and re-layouts  25 us (2%)
  between operations  15.9 us (1%)
    reduce_scatter x7, waiting for transfers between devices, scatter_grad(): lax.psum_scatter(grad.astype(jnp.bfloat16), axis_name, scatter_dimension=...  361 us
    all_gather x4, waiting for transfers between devices, sum_parts(): lax.all_gather(own, axis_name, axis=0, tiled=True).astype(jnp.float32)  180 us
    reduce_scatter x4, waiting for transfers between devices, sum_parts(): lax.psum_scatter(part.astype(jnp.bfloat16), axis_name, scatter_dimension=...  130 us
    all_gather x1, waiting for transfers between devices, on_device(): lax.all_gather(w_gate, 'dp', axis=0, tiled=True)  48.9 us
    all_gather x1, waiting for transfers between devices, on_device(): lax.all_gather(w_down, 'dp', axis=1, tiled=True)  47 us
    all_gather x1, waiting for transfers between devices, on_device(): lax.all_gather(w_up, 'dp', axis=0, tiled=True)  45.7 us
    all_gather x1, waiting for transfers between devices, on_device(): lax.all_gather(w_query, 'dp', axis=0, tiled=True)  26.1 us
    all_gather x1, waiting for transfers between devices, on_device(): lax.all_gather(w_key, 'dp', axis=0, tiled=True)  26 us
  transfers between devices with their start and end apart: 22, of which 20 were waited for; matrix products, arithmetic and copies ran while one was open for 10% of the time, Pallas kernels for 0%

commit v1 on v0

--- a/solution.py
+++ b/solution.py
@@ -7,6 +7,13 @@
 HD = 128
 EPS = 1e-06
 THETA = 500000.0
+
+
+def all_by_exchange(block, axis, dim):
+    peers = lax.axis_size(axis)
+    tiles = jnp.stack([block for _ in range(peers)])
+    tiles = lax.all_to_all(tiles, axis, split_axis=0, concat_axis=0)
+    return jnp.concatenate(tiles, axis=dim)
 
 
 def doc_positions(seg_row):
@@ -113,7 +120,7 @@
 
 def sum_parts(part, axis_name):
     own = lax.psum_scatter(part.astype(jnp.bfloat16), axis_name, scatter_dimension=0, tiled=True)
-    return lax.all_gather(own, axis_name, axis=0, tiled=True).astype(jnp.float32)
+    return all_by_exchange(own, axis_name, 0).astype(jnp.float32)
 
 
 def norm_back(raw, inv_scale, gained, row_sums, width):

time: 1180 us -> 1110 us (0.941)
  waiting for transfers between devices: 891 us -> 742 us
  blocking collectives: 44.9 us -> 97.3 us
  starting transfers between devices: 2.11 us -> 15.4 us
    all_gather x4 -> x0, waiting for transfers between devices: 180 us -> none  [sum_parts(): lax.all_gather(own, axis_name, axis=0, tiled=True).astype(jnp.float32)]
    all_to_all x0 -> x3, waiting for transfers between devices: none -> 95.1 us  [all_by_exchange(): tiles = lax.all_to_all(tiles, axis, split_axis=0, concat_axis=0)]
    all_to_all x0 -> x1, blocking collectives: none -> 51.2 us  [all_by_exchange(): tiles = lax.all_to_all(tiles, axis, split_axis=0, concat_axis=0)]
    all_gather x1, waiting for transfers between devices: 48.9 us -> 0.01 us  [on_device(): lax.all_gather(w_gate, 'dp', axis=0, tiled=True)]
    all_to_all x0 -> x3, starting transfers between devices: none -> 13.5 us  [all_by_exchange(): tiles = lax.all_to_all(tiles, axis, split_axis=0, concat_axis=0)]
  transfers between devices with their start and end apart: 22 -> 21, of which waited for: 20 -> 17; matrix products, arithmetic and copies ran while one was open for 10% -> 11% of each run, Pallas kernels for 0% -> 0%
where the time goes in v1:
time: 1110 us; the launch traced here: 1100 us
  waiting for transfers between devices  742 us (67%)
  matrix products  137 us (12%)
  blocking collectives  97.3 us (9%)
  other arithmetic  59.6 us (5%)
  local copies, waits for them, and re-layouts  36.2 us (3%)
  between operations  15.9 us (1%)
  starting transfers between devices  15.4 us (1%)
    reduce_scatter x7, waiting for transfers between devices, scatter_grad(): lax.psum_scatter(grad.astype(jnp.bfloat16), axis_name, scatter_dimension=...  351 us
    reduce_scatter x4, waiting for transfers between devices, sum_parts(): lax.psum_scatter(part.astype(jnp.bfloat16), axis_name, scatter_dimension=...  128 us
    all_to_all x3, waiting for transfers between devices, all_by_exchange(): tiles = lax.all_to_all(tiles, axis, split_axis=0, concat_axis=0)  95.1 us
    all_to_all x1, blocking collectives, all_by_exchange(): tiles = lax.all_to_all(tiles, axis, split_axis=0, concat_axis=0)  51.2 us
    all_gather x1, waiting for transfers between devices, on_device(): lax.all_gather(w_down, 'dp', axis=1, tiled=True)  47 us
    all_gather x1, waiting for transfers between devices, on_device(): lax.all_gather(w_up, 'dp', axis=0, tiled=True)  43.4 us
    all_gather x1, waiting for transfers between devices, on_device(): lax.all_gather(w_query, 'dp', axis=0, tiled=True)  26.1 us
    all_gather x1, waiting for transfers between devices, on_device(): lax.all_gather(w_key, 'dp', axis=0, tiled=True)  26 us
  transfers between devices with their start and end apart: 21, of which 17 were waited for; matrix products, arithmetic and copies ran while one was open for 11% of the time, Pallas kernels for 0%

profile of v1, /device:TPU:0, one launch (start us, length us, event | category | flops | bytes accessed | tf_op | source)
XLA Modules:
  0.0 1103.7 jit_solution(4844566471739694240)
XLA Ops:
  14.4 26.0 %all-gather.12.cloned.1.call-done = bf16[2048,512]{1,0:T(8,128)(2,1)} async-done(((bf16[256,512]{1,0:T(8,128)(2,1)}), bf16[2048,512]{1,0:T(8,128)(2,1)}) %all-gather.12.cloned.1.call-update) | async-done | bytes 2097168 | tf_op jit(solution)/shard_map/all_gather | solution.py:149
  40.4 3.5 multiply_reduce_fusion.3
  44.0 26.1 %all-gather.10.cloned.1.call-done = bf16[2048,512]{1,0:T(8,128)(2,1)} async-done(((bf16[256,512]{1,0:T(8,128)(2,1)}), bf16[2048,512]{1,0:T(8,128)(2,1)}) %all-gather.10.cloned.1.call-update) | async-done | bytes 2097168 | tf_op jit(solution)/shard_map/all_gather | solution.py:148
  70.1 3.5 multiply_reduce_fusion.4
  73.7 11.7 %all-reduce.2 = (f32[512]{0:T(512)S(1)}, f32[512]{0:T(512)S(1)}) all-reduce(f32[512]{0:T(512)S(1)} %get-tuple-element.81, f32[512]{0:T(512)S(1)} %get-tuple-element.83), channel_id=1, replica_groups=mesh['dp'=8,'mp'=4] {'mp'}, use_global_device_ids=true, to_apply=%region_5.6 | all-reduce | flops 1024 | bytes 8192 | tf_op jit(solution)/shard_map/psum | solution.py:168
  86.6 2.4 copy.82
  88.9 2.4 copy.81
  93.9 2.4 copy.79
  96.2 2.3 subtract_convert_fusion.3
  100.0 2.0 copy-done.3
  103.0 3.0 convolution_convert_fusion.10
  108.2 21.4 %all-gather.14.cloned.1.call-done = bf16[512,2048]{1,0:T(8,128)(2,1)} async-done(((bf16[512,256]{1,0:T(8,128)(2,1)}), bf16[512,2048]{1,0:T(8,128)(2,1)}) %all-gather.14.cloned.1.call-update) | async-done | bytes 2097168 | tf_op jit(solution)/shard_map/all_gather | solution.py:151
  129.7 4.2 convolution_convert_fusion.8
  136.5 41.2 %reduce-scatter.12.cloned.1.call-done = bf16[128,2048]{1,0:T(8,128)(2,1)} async-done(((bf16[512,2048]{1,0:T(8,128)(2,1)}), bf16[128,2048]{1,0:T(8,128)(2,1)}) %reduce-scatter.12.cloned.1.call-update) | async-done | bytes 524304 | tf_op jit(solution)/shard_map/reduce_scatter | solution.py:122
  179.0 51.2 %all_to_all.20 = bf16[4,128,2048]{2,1,0:T(8,128)(2,1)S(1)} all-to-all(bf16[4,128,2048]{2,1,0:T(8,128)(2,1)S(1)} %stack.8), channel_id=1, replica_groups=mesh['dp'=8,'mp'=4] {'mp'}, dimensions={0} | all-to-all | bytes 4194304 | tf_op jit(solution)/shard_map/all_to_all | solution.py:15
  230.6 4.4 fusion.22
  235.1 10.6 fusion.44
  245.7 43.4 %all-gather.18.cloned.1.call-done = bf16[2048,2048]{1,0:T(8,128)(2,1)} async-done(((bf16[256,2048]{1,0:T(8,128)(2,1)}), bf16[2048,2048]{1,0:T(8,128)(2,1)}) %all-gather.18.cloned.1.call-update) | async-done | bytes 8388624 | tf_op jit(solution)/shard_map/all_gather | solution.py:153
  289.1 10.8 multiply_convert_fusion.3
  299.9 47.0 %all-gather.20.cloned.1.call-done = bf16[2048,2048]{1,0:T(8,128)(2,1)} async-done(((bf16[2048,256]{1,0:T(8,128)(2,1)}), bf16[2048,2048]{1,0:T(8,128)(2,1)}) %all-gather.20.cloned.1.call-update) | async-done | bytes 8388624 | tf_op jit(solution)/shard_map/all_gather | solution.py:154
  346.9 9.8 convolution_convert_fusion.7
  356.7 43.8 %reduce-scatter.14.cloned.1.call-done = bf16[128,2048]{1,0:T(8,128)(2,1)} async-done(((bf16[512,2048]{1,0:T(8,128)(2,1)}), bf16[128,2048]{1,0:T(8,128)(2,1)}) %reduce-scatter.14.cloned.1.call-update) | async-done | bytes 524304 | tf_op jit(solution)/shard_map/reduce_scatter | solution.py:122
  400.5 2.6 stack.9
  403.1 4.4 all-to-all-start.1
  408.4 47.3 %all-to-all-done.1 = bf16[4,128,2048]{2,1,0:T(8,128)(2,1)} async-done(((bf16[4,128,2048]{2,1,0:T(8,128)(2,1)}), bf16[4,128,2048]{2,1,0:T(8,128)(2,1)}, u32[]{:S(2)}, u32[]{:S(2)}) %all-to-all-start.1) | async-done | bytes 2097184 | tf_op jit(solution)/shard_map/all_to_all | solution.py:15
  455.7 2.1 fusion
  457.8 3.2 fusion.10
  461.0 2.8 fusion.7
  463.9 12.3 %multiply_convert_fusion.1 = (bf16[512,2048]{1,0:T(8,128)(2,1)}, bf16[512,2048]{1,0:T(8,128)(2,1)}) fusion(f32[512,2048]{1,0:T(8,128)S(1)} %copy-done.42, f32[512,2048]{1,0:T(8,128)} %get-tuple-element.88, bf16[512,2048]{1,0:T(8,128)(2,1)S(1)} %fusion.7, bf16[2048,2048]{1,0:T(8,128)(2,1)} %all-gather.20.cloned.1.call-done), kind=kOutput, calls=%fused_computation.38 | convolution fusion | flops 4308598784 | bytes 23068672 | tf_op jit(solution)/shard_map/dot_general | solution.py:199
  476.2 7.8 fusion.45
  483.9 9.4 add_convert_fusion.1
  493.4 42.8 %reduce-scatter.16.cloned.1.call-done = bf16[128,2048]{1,0:T(8,128)(2,1)} async-done(((bf16[512,2048]{1,0:T(8,128)(2,1)}), bf16[128,2048]{1,0:T(8,128)(2,1)}) %reduce-scatter.16.cloned.1.call-update) | async-done | bytes 524304 | tf_op jit(solution)/shard_map/reduce_scatter | solution.py:122
  536.2 2.6 stack.10
  538.8 4.5 all-to-all-start.2
  543.6 47.9 %all-to-all-done.2 = bf16[4,128,2048]{2,1,0:T(8,128)(2,1)} async-done(((bf16[4,128,2048]{2,1,0:T(8,128)(2,1)}), bf16[4,128,2048]{2,1,0:T(8,128)(2,1)}, u32[]{:S(2)}, u32[]{:S(2)}) %all-to-all-start.2) | async-done | bytes 2097184 | tf_op jit(solution)/shard_map/all_to_all | solution.py:15
  591.5 4.4 fusion.19
  596.0 5.6 fusion.16
  604.5 2.2 convolution_convert_fusion.11
  613.9 2.5 copy.63
  618.0 2.9 pad_maximum_fusion
  620.9 2.5 copy.59
  625.2 10.2 all-reduce.1
  642.5 2.6 add_convert_fusion
  645.2 4.2 convolution_convert_fusion.3
  649.6 4.3 fusion.24
  654.0 4.2 fusion.23
  658.3 4.2 fusion.25
  662.7 10.1 convolution_convert_fusion
  672.9 10.0 convolution_convert_fusion.1
  683.2 10.1 convolution_convert_fusion.2
  693.3 2.6 stack.11
  695.9 4.5 all-to-all-start.3
  700.5 24.2 %all-reduce = (f32[512]{0:T(512)}, f32[512]{0:T(512)}, f32[2048]{0:T(1024)}, f32[2048]{0:T(1024)}) all-reduce(f32[512]{0:T(512)S(1)} %get-tuple-element.45, f32[512]{0:T(512)S(1)} %get-tuple-element.43, f32[2048]{0:T(1024)S(1)} %get-tuple-element.39, f32[2048]{0:T(1024)S(1)} %get-tuple-element.41), channel_id=1, replica_groups=mesh['dp'=8,'mp'=4] {'dp'}, use_global_device_ids=true, to_apply=%region_29.30 | all-reduce | flops 5120 | bytes 40960 | tf_op jit(solution)/shard_map/psum | solution.py:257
  724.7 6.1 reduce-scatter.26.cloned.1.call-done
  732.6 42.6 %reduce-scatter.22.cloned.1.call-done = bf16[256,512]{0,1:T(8,128)(2,1)} async-done(((bf16[2048,512]{0,1:T(8,128)(2,1)}), bf16[256,512]{0,1:T(8,128)(2,1)}) %reduce-scatter.22.cloned.1.call-update) | async-done | bytes 262160 | tf_op jit(solution)/shard_map/reduce_scatter | solution.py:115
  777.1 42.4 %reduce-scatter.20.cloned.1.call-done = bf16[256,512]{0,1:T(8,128)(2,1)} async-done(((bf16[2048,512]{0,1:T(8,128)(2,1)}), bf16[256,512]{0,1:T(8,128)(2,1)}) %reduce-scatter.20.cloned.1.call-update) | async-done | bytes 262160 | tf_op jit(solution)/shard_map/reduce_scatter | solution.py:115
  821.4 42.4 %reduce-scatter.24.cloned.1.call-done = bf16[256,512]{0,1:T(8,128)(2,1)} async-done(((bf16[2048,512]{0,1:T(8,128)(2,1)}), bf16[256,512]{0,1:T(8,128)(2,1)}) %reduce-scatter.24.cloned.1.call-update) | async-done | bytes 262160 | tf_op jit(solution)/shard_map/reduce_scatter | solution.py:115
  865.7 72.8 %reduce-scatter.32.cloned.1.call-done = bf16[2048,256]{1,0:T(8,128)(2,1)} async-done(((bf16[2048,2048]{1,0:T(8,128)(2,1)}), bf16[2048,256]{1,0:T(8,128)(2,1)}) %reduce-scatter.32.cloned.1.call-update) | async-done | bytes 1048592 | tf_op jit(solution)/shard_map/reduce_scatter | solution.py:115
  938.5 2.7 convert_element_type.226
  941.2 72.2 %reduce-scatter.30.cloned.1.call-done = bf16[256,2048]{1,0:T(8,128)(2,1)} async-done(((bf16[2048,2048]{1,0:T(8,128)(2,1)}), bf16[256,2048]{1,0:T(8,128)(2,1)}) %reduce-scatter.30.cloned.1.call-update) | async-done | bytes 1048592 | tf_op jit(solution)/shard_map/reduce_scatter | solution.py:115
  1013.3 2.8 convert_element_type.224
  1016.1 72.1 %reduce-scatter.28.cloned.1.call-done = bf16[256,2048]{1,0:T(8,128)(2,1)} async-done(((bf16[2048,2048]{1,0:T(8,128)(2,1)}), bf16[256,2048]{1,0:T(8,128)(2,1)}) %reduce-scatter.28.cloned.1.call-update) | async-done | bytes 1048592 | tf_op jit(solution)/shard_map/reduce_scatter | solution.py:115
  1088.2 2.8 convert_element_type.222
  1091.0 5.7 convert_add_fusion
  (174 shorter events, 49.1 us)
Async XLA Ops:
  7.2 33.2 %all-gather.12.cloned.1.call-start = ((), (), s32[]{:S(2)}) async-start(), calls=%async_computation.17 | async-start | bytes 2359296 | tf_op jit(solution)/shard_map/all_gather | solution.py:149
  7.9 62.2 %all-gather.10.cloned.1.call-start = ((), (), s32[]{:S(2)}) async-start(), calls=%async_computation.16 | async-start | bytes 2359296 | tf_op jit(solution)/shard_map/all_gather | solution.py:148
  8.7 94.3 %all-gather.8.cloned.1.call-start = ((), (), s32[]{:S(2)}) async-start(), calls=%async_computation.15 | async-start | bytes 2359296 | tf_op jit(solution)/shard_map/all_gather | solution.py:150
  9.4 120.3 %all-gather.14.cloned.1.call-start = ((), (), s32[]{:S(2)}) async-start(), calls=%async_computation.18 | async-start | bytes 2359296 | tf_op jit(solution)/shard_map/all_gather | solution.py:151
  10.0 167.7 %reduce-scatter.12.cloned.1.call-start = ((), (), s32[]{:S(2)}) async-start(), calls=%async_computation.19 | async-start | bytes 2621440 | tf_op jit(solution)/shard_map/reduce_scatter | solution.py:122
  43.9 41.4 %copy-start.35 = (f32[512]{0:T(512)S(1)}, f32[512]{0:T(512)}, u32[]{:S(2)}) copy-start(f32[512]{0:T(512)} %param.27) | copy-start | bytes 6148
  73.6 17.8 %copy-start.6 = (f32[512,512]{0,1:T(8,128)}, f32[512,512]{0,1:T(8,128)S(1)}, u32[]{:S(2)}) copy-start(f32[512,512]{0,1:T(8,128)S(1)} %get-tuple-element.84) | copy-start | bytes 3145732
  73.6 17.6 %copy-start.34 = (f32[512]{0:T(512)S(1)}, f32[512]{0:T(512)}, u32[]{:S(2)}) copy-start(f32[512]{0:T(512)} %param.26) | copy-start | bytes 6148
  91.4 4.8 copy-start.17
  98.5 4.4 copy-start.9
  98.5 4.4 copy-start.11
  98.5 4.4 copy-start.13
  98.5 4.4 copy-start.15
  98.6 4.4 copy-start.7
  100.0 2.0 copy-start.3
  103.0 3.9 copy-start.4
  108.2 26.2 %copy-start.37 = (bf16[4,128,512]{2,1,0:T(8,128)(2,1)}, bf16[4,128,512]{2,1,0:T(8,128)(2,1)S(1)}, u32[]{:S(2)}) copy-start(bf16[4,128,512]{2,1,0:T(8,128)(2,1)S(1)} %convolution_convert_fusion.12) | copy-start | bytes 1572868
  133.9 101.2 %all-gather.16.cloned.1.call-start = ((), (), s32[]{:S(2)}) async-start(), calls=%async_computation.20 | async-start | bytes 9437184 | tf_op jit(solution)/shard_map/all_gather | solution.py:152
  134.5 154.6 %all-gather.18.cloned.1.call-start = ((), (), s32[]{:S(2)}) async-start(), calls=%async_computation.21 | async-start | bytes 9437184 | tf_op jit(solution)/shard_map/all_gather | solution.py:153
  135.2 211.6 %all-gather.20.cloned.1.call-start = ((), (), s32[]{:S(2)}) async-start(), calls=%async_computation.22 | async-start | bytes 9437184 | tf_op jit(solution)/shard_map/all_gather | solution.py:154
  136.0 94.6 %copy-start.32 = (f32[2048]{0:T(1024)S(1)}, f32[2048]{0:T(1024)}, u32[]{:S(2)}) copy-start(f32[2048]{0:T(1024)} %param.28) | copy-start | bytes 24580
  136.0 264.5 %reduce-scatter.14.cloned.1.call-start = ((), (), s32[]{:S(2)}) async-start(), calls=%async_computation.23 | async-start | bytes 2621440 | tf_op jit(solution)/shard_map/reduce_scatter | solution.py:122
  230.1 5.0 copy-start.1
  235.1 54.0 %copy-start.25 = (bf16[512,2048]{1,0:T(8,128)(2,1)S(1)}, bf16[512,2048]{1,0:T(8,128)(2,1)}, u32[]{:S(2)}) copy-start(bf16[512,2048]{1,0:T(8,128)(2,1)} %fusion.22) | copy-start | bytes 6291460
  356.7 101.1 %copy-start = (bf16[512,2048]{1,0:T(8,128)(2,1)S(1)}, bf16[512,2048]{1,0:T(8,128)(2,1)}, u32[]{:S(2)}) copy-start(bf16[512,2048]{1,0:T(8,128)(2,1)} %param.16) | copy-start | bytes 6291460
  356.7 101.1 %copy-start.33 = (f32[2048]{0:T(1024)S(1)}, f32[2048]{0:T(1024)}, u32[]{:S(2)}) copy-start(f32[2048]{0:T(1024)} %param.29) | copy-start | bytes 24580
  403.1 52.6 %all-to-all-start.1 = ((bf16[4,128,2048]{2,1,0:T(8,128)(2,1)}), bf16[4,128,2048]{2,1,0:T(8,128)(2,1)}, u32[]{:S(2)}, u32[]{:S(2)}) async-start(bf16[4,128,2048]{2,1,0:T(8,128)(2,1)} %stack.9), calls=%async_computation.3 | async-start | bytes 4194304 | tf_op jit(solution)/shard_map/all_to_all | solution.py:15
  407.6 128.6 %reduce-scatter.16.cloned.1.call-start = ((), (), s32[]{:S(2)}) async-start(), calls=%async_computation.24 | async-start | bytes 2621440 | tf_op jit(solution)/shard_map/reduce_scatter | solution.py:122
  461.0 2.9 copy-start.42
  463.8 12.3 %copy-start.26 = (bf16[512,2048]{1,0:T(8,128)(2,1)}, bf16[512,2048]{1,0:T(8,128)(2,1)S(1)}, u32[]{:S(2)}) copy-start(bf16[512,2048]{1,0:T(8,128)(2,1)S(1)} %fusion.7) | copy-start | bytes 6291460
  476.2 7.8 copy-start.43
  538.8 52.7 %all-to-all-start.2 = ((bf16[4,128,2048]{2,1,0:T(8,128)(2,1)}), bf16[4,128,2048]{2,1,0:T(8,128)(2,1)}, u32[]{:S(2)}, u32[]{:S(2)}) async-start(bf16[4,128,2048]{2,1,0:T(8,128)(2,1)} %stack.10), calls=%async_computation.5 | async-start | bytes 4194304 | tf_op jit(solution)/shard_map/all_to_all | solution.py:15
  543.3 150.0 %reduce-scatter.18.cloned.1.call-start = ((), (), s32[]{:S(2)}) async-start(), calls=%async_computation.25 | async-start | bytes 2621440 | tf_op jit(solution)/shard_map/reduce_scatter | solution.py:122
  591.5 4.4 copy-start.2
  591.5 4.4 copy-start.8
  595.9 5.6 copy-start.36
  596.0 5.6 copy-start.38
  601.5 5.1 copy-start.29
  601.5 2.9 copy-start.5
  602.9 3.7 copy-start.41
  606.6 1.7 copy-start.14
  606.6 1.7 copy-start.16
  608.3 1.0 copy-start.10
  608.3 1.2 copy-start.12
  608.3 2.2 copy-start.22
  608.4 2.2 copy-start.23
  635.5 3.6 copy-start.27
  637.4 3.0 copy-start.18
  639.1 1.3 copy-start.20
  639.1 1.8 copy-start.28
  640.9 1.6 copy-start.24
  640.9 1.7 copy-start.30
  642.5 2.7 copy-start.39
  645.2 4.4 copy-start.21
  645.2 85.6 %reduce-scatter.26.cloned.1.call-start = ((), (), s32[]{:S(2)}) async-start(), calls=%async_computation.29 | async-start | bytes 2359296 | tf_op jit(solution)/shard_map/reduce_scatter | solution.py:115
  649.5 4.5 copy-start.19
  649.5 125.7 %reduce-scatter.22.cloned.1.call-start = ((), (), s32[]{:S(2)}) async-start(), calls=%async_computation.27 | async-start | bytes 2359296 | tf_op jit(solution)/shard_map/reduce_scatter | solution.py:115
  653.9 4.3 copy-start.31
  653.9 165.6 %reduce-scatter.20.cloned.1.call-start = ((), (), s32[]{:S(2)}) async-start(), calls=%async_computation.26 | async-start | bytes 2359296 | tf_op jit(solution)/shard_map/reduce_scatter | solution.py:115
  658.2 205.6 %reduce-scatter.24.cloned.1.call-start = ((), (), s32[]{:S(2)}) async-start(), calls=%async_computation.28 | async-start | bytes 2359296 | tf_op jit(solution)/shard_map/reduce_scatter | solution.py:115
  662.5 275.9 %reduce-scatter.32.cloned.1.call-start = ((), (), s32[]{:S(2)}) async-start(), calls=%async_computation.32 | async-start | bytes 9437184 | tf_op jit(solution)/shard_map/reduce_scatter | solution.py:115
  672.8 340.5 %reduce-scatter.30.cloned.1.call-start = ((), (), s32[]{:S(2)}) async-start(), calls=%async_computation.31 | async-start | bytes 9437184 | tf_op jit(solution)/shard_map/reduce_scatter | solution.py:115
  682.9 405.2 %reduce-scatter.28.cloned.1.call-start = ((), (), s32[]{:S(2)}) async-start(), calls=%async_computation.30 | async-start | bytes 9437184 | tf_op jit(solution)/shard_map/reduce_scatter | solution.py:115
  695.9 395.0 %all-to-all-start.3 = ((bf16[4,128,2048]{2,1,0:T(8,128)(2,1)}), bf16[4,128,2048]{2,1,0:T(8,128)(2,1)}, u32[]{:S(2)}, u32[]{:S(2)}) async-start(bf16[4,128,2048]{2,1,0:T(8,128)(2,1)} %stack.11), calls=%async_computation.7 | async-start | bytes 4194304 | tf_op jit(solution)/shard_map/all_to_all | solution.py:15
  (1 other events, 0.8 us)
Sparse Core Ops, SparseCore 0:
  9.9 30.4 all-gather.11
  42.3 27.7 all-gather.9
  72.0 27.7 all-gather.7
  101.5 28.0 all-gather.13
  134.0 43.6 reduce-scatter.11
  179.4 53.4 all-gather.15
  234.8 54.2 all-gather.17
  291.0 55.8 all-gather.19
  356.8 43.6 reduce-scatter.13
  493.5 42.6 reduce-scatter.15
  645.3 41.7 reduce-scatter.17
  690.2 40.5 reduce-scatter.25
  734.1 41.0 reduce-scatter.21
  778.4 41.1 reduce-scatter.19
  822.6 41.1 reduce-scatter.23
  867.1 71.2 reduce-scatter.31
  941.8 71.5 reduce-scatter.29
  1016.6 71.4 reduce-scatter.27
